TPU v7x, 8 devices: a whole 2x2x1 slice. The times are simulated.
8 devices in a mesh: dp: 1 (over z), sp: 8 (over x, y, core).
Axes of the slice: x: 2, y: 2, z: 1, core: 2. Of those that a mesh axis runs over, the one named last changes fastest.
Arguments:
- q: bfloat16 [32, 16, 256], P('dp')
- k: bfloat16 [32, 8192, 1, 256], P('dp', 'sp')
- v: bfloat16 [32, 8192, 1, 256], P('dp', 'sp')
Outputs:
- q: bfloat16 [32, 16, 256], P('dp')
All inputs are finite; a program needn't handle non-finite values.
Results may differ from a plain program's by a relative error of at most 0.012.
Values are sent between devices in bfloat16 or wider.
A program may use at most 2 GiB of HBM per device.

v0:
```python
import jax
import jax.numpy as jnp
from jax import lax
from jax.sharding import PartitionSpec as P


def einsum(form, a, b):
    return jnp.einsum(form, a.astype(jnp.float32), b.astype(jnp.float32))


def part_of(q, k, v):
    grouped = q.reshape(q.shape[0], k.shape[2], -1, q.shape[2])
    scores = einsum("bgsd,bugd->bgsu", grouped, k) * q.shape[2] ** -0.5
    high = jnp.max(scores, -1, keepdims=True)
    weights = jnp.exp(scores - high)
    seen = einsum("bgsu,bugd->bgsd", weights.astype(jnp.bfloat16), v)
    return jnp.concatenate([seen, jnp.sum(weights, -1, keepdims=True), high], -1)


def together(parts):
    seen, total, high = parts[..., :-2], parts[..., -2:-1], parts[..., -1:]
    scale = jnp.exp(high - jnp.max(high, 0))
    return (jnp.sum(seen * scale, 0) / jnp.sum(total * scale, 0)).astype(jnp.bfloat16)


def solution(mesh):
    def step(q, k, v):
        return together(lax.all_gather(part_of(q, k, v), "sp")).reshape(q.shape)

    return jax.shard_map(
        step,
        mesh=mesh,
        in_specs=(P("dp", None, None), P("dp", "sp", None, None), P("dp", "sp", None, None)),
        out_specs=P("dp", None, None),
        check_vma=False,
    )
```

profile of v0, /device:TPU:0, one launch (start us, length us, event | category | flops | bytes accessed | tf_op | source)
XLA Modules:
  0.0 89.0 jit_solution(9281261428524906462)
XLA Ops:
  6.5 0.0 copy-start
  6.5 0.0 all-gather.3.cloned.1.call-start
  6.5 0.9 %copy-done = bf16[32,16,256]{2,1,0:T(8,128)(2,1)S(1)} copy-done((bf16[32,16,256]{2,1,0:T(8,128)(2,1)S(1)}, bf16[32,16,256]{2,1,0:T(8,128)(2,1)}, u32[]{:S(2)}) %copy-start) | copy-done | bytes 262168
  7.5 10.3 %multiply_reduce_fusion = (f32[32,16]{1,0:T(8,128)S(1)}, f32[32,16,1024]{2,1,0:T(8,128)S(1)}) fusion(bf16[32,16,256]{2,1,0:T(8,128)(2,1)S(1)} %copy-done, bf16[32,1024,1,256]{3,1,2,0:T(8,128)(2,1)} %param.4), kind=kOutput, calls=%fused_computation.7 | convolution fusion | flops 269483520 | bytes 19138560 | tf_op jit(solution)/shard_map/bgsd,bugd->bgsu/dot_general | solution.py:8
  17.8 0.5 fusion.5
  18.3 8.1 %fusion.7 = f32[32,1,16,256]{3,2,0,1:T(8,128)S(1)} fusion(bf16[32,1024,1,256]{3,1,2,0:T(8,128)(2,1)} %param.5, f32[32,16,1024]{2,1,0:T(8,128)S(1)} %get-tuple-element.11, f32[32,16]{1,0:T(8,128)S(1)} %get-tuple-element.10), kind=kOutput, calls=%fused_computation.10 | convolution fusion | flops 270008320 | bytes 19400704 | tf_op jit(solution)/shard_map/bgsu,bugd->bgsd/dot_general | solution.py:8
  26.4 0.3 copy.27
  26.7 0.3 copy.28
  27.0 1.0 %maximum_bitcast_fusion = f32[32,1,16,258]{3,2,1,0:T(8,128)} fusion(f32[32,1,16,1]{3,2,0,1:T(8,128)S(1)} %copy.28, f32[32,1,16,1]{3,2,0,1:T(8,128)S(1)} %copy.27, f32[32,1,16,256]{3,2,0,1:T(8,128)S(1)} %fusion.7), kind=kLoop, calls=%fused_computation.13 | loop fusion | flops 264192 | bytes 1056768 | tf_op jit(solution)/shard_map/concatenate | solution.py:17
  28.0 0.0 all-gather.3.cloned.1.call-update
  28.0 42.5 %all-gather.3.cloned.1.call-done = f32[256,1,16,258]{3,2,1,0:T(8,128)} async-done(((f32[32,1,16,258]{3,2,1,0:T(8,128)}), f32[256,1,16,258]{3,2,1,0:T(8,128)}) %all-gather.3.cloned.1.call-update) | async-done | bytes 4227088 | tf_op jit(solution)/shard_map/all_gather | solution.py:28
  70.6 4.4 %fusion.15 = (f32[8,32,1,16,1]{4,3,1,0,2:T(8,128)}, f32[32,16]{1,0:T(8,128)S(1)}, f32[8,32,1,16,1]{4,3,1,0,2:T(8,128)S(1)}) fusion(f32[8,32,1,16,258]{4,3,1,0,2:T(8,128)} %bitcast.20), kind=kLoop, calls=%fused_computation.20 | loop fusion | flops 3584 | bytes 67584 | tf_op jit(solution)/shard_map/slice | solution.py:21
  75.0 2.4 %copy.39 = f32[8,32,1,16,1]{1,3,4,2,0:T(8,128)S(1)} copy(f32[8,32,1,16,1]{4,3,1,0,2:T(8,128)} %get-tuple-element.5) | data formatting | bytes 32768
  77.4 0.1 copy.40
  77.5 0.9 %copy.38 = f32[8,32,1,16,1]{1,3,4,2,0:T(8,128)S(1)} copy(f32[8,32,1,16,1]{4,3,1,0,2:T(8,128)S(1)} %get-tuple-element.7) | data formatting | bytes 32768
  78.5 0.1 copy.33
  78.5 0.1 copy.31
  78.6 2.7 %fusion.4 = f32[32,16,256]{2,1,0:T(8,128)S(1)} fusion(f32[8,32,1,16,258]{4,3,1,0,2:T(8,128)} %bitcast.21, f32[8,32,16]{2,1,0:T(8,128)S(1)} %copy.31), kind=kLoop, calls=%fused_computation.5 | loop fusion | flops 1966080 | bytes 4734976 | tf_op jit(solution)/shard_map/reduce_sum | solution.py:23
  81.3 0.8 divide_convert_fusion
  (1 shorter events, 0.0 us)
Async XLA Ops:
  6.5 1.0 %copy-start = (bf16[32,16,256]{2,1,0:T(8,128)(2,1)S(1)}, bf16[32,16,256]{2,1,0:T(8,128)(2,1)}, u32[]{:S(2)}) copy-start(bf16[32,16,256]{2,1,0:T(8,128)(2,1)} %param.3) | copy-start | bytes 786436
  6.5 64.0 %all-gather.3.cloned.1.call-start = ((), (), s32[]{:S(2)}) async-start(), calls=%async_computation | async-start | bytes 7077888 | tf_op jit(solution)/shard_map/all_gather | solution.py:28
Sparse Core Ops, SparseCore 0:
  28.2 42.3 all-gather.2
where the time goes:
time: 89.2 us; the launch traced here: 89 us
  waiting for transfers between devices  42.5 us (48%)
  matrix products  18.4 us (21%)
  between operations  13.4 us (15%)
  other arithmetic  9.56 us (11%)
  local copies, waits for them, and re-layouts  5.08 us (6%)
    all_gather x1, waiting for transfers between devices, step(): return together(lax.all_gather(part_of(q, k, v), 'sp')).reshape(q.shape)  42.5 us
    dot_general x2, matrix products, einsum(): return jnp.einsum(form, a.astype(jnp.float32), b.astype(jnp.float32))  18.4 us
    slice x1, other arithmetic, together(): seen, total, high = (parts[..., :-2], parts[..., -2:-1], parts[..., -1:])  4.43 us
    unnamed x5, local copies, waits for them, and re-layouts  4.38 us
    reduce_sum x1, other arithmetic, together(): jnp.sum(seen * scale, 0) / jnp.sum(total * scale, 0)  2.69 us
  transfers between devices with their start and end apart: 1, of which 1 were waited for; matrix products, arithmetic and copies ran while one was open for 0% of the time, Pallas kernels for 0%

commit v1 on v0

v1 whole, which is shorter than its diff:
```python
import functools

import jax
import jax.numpy as jnp
from jax import lax
from jax.experimental import pallas as pl
from jax.experimental.pallas import tpu as pltpu
from jax.sharding import PartitionSpec as P

MESH = pl.DeviceIdType.MESH
F32 = jnp.float32
BF16 = jnp.bfloat16
AHEAD = 4


def kernel(n, scale, q_hbm, k_hbm, v_hbm, o_ref, q_buf, k_buf, v_buf, part, sent, stat, got, got_stat, out,
           q_sem, k_sem, v_sem, send_sem, send_stat_sem, got_sem, got_stat_sem, out_sem):
    me = lax.axis_index("sp")
    batch, heads, head = q_buf.shape
    groups = batch // n

    def peer(r):
        return lax.rem(me + r, n)

    def k_copy(s):
        return pltpu.make_async_copy(k_hbm.at[s], k_buf.at[s], k_sem.at[s])

    def v_copy(s):
        return pltpu.make_async_copy(v_hbm.at[s], v_buf.at[s], v_sem.at[s])

    q_copy = pltpu.make_async_copy(q_hbm, q_buf, q_sem)
    k_copy(0).start()
    q_copy.start()
    for s in range(AHEAD):
        if s > 0:
            k_copy(s).start()
        v_copy(s).start()

    barrier = pltpu.get_barrier_semaphore()
    for r in range(1, n):
        pl.semaphore_signal(barrier, inc=1, device_id={"sp": peer(r)}, device_id_type=MESH)

    def scores_of(s):
        return lax.dot_general(q_buf[s], k_buf[s], (((1,), (1,)), ((), ())), preferred_element_type=F32)

    def finish(s, scores):
        high = jnp.max(scores, -1, keepdims=True)
        weights = jnp.exp((scores - high) * scale)
        total = jnp.sum(weights, -1, keepdims=True)
        seen = jnp.dot(weights.astype(BF16), v_buf[s], preferred_element_type=F32)
        part[s] = seen
        sent[s] = seen.astype(BF16)
        lane = lax.broadcasted_iota(jnp.int32, (heads, 128), 1)
        both = jnp.where(lane == 0, high * scale, total)
        stat[s, :, :heads] = jnp.transpose(both)[:2]

    def send(s):
        owner = lax.rem(s, n)
        group = s // n
        slot = lax.rem(me - owner + n, n) - 1

        @pl.when(owner != me)
        def _():
            pltpu.make_async_remote_copy(
                src_ref=sent.at[s], dst_ref=got.at[group, slot], send_sem=send_sem, recv_sem=got_sem.at[group],
                device_id={"sp": owner}, device_id_type=MESH).start()
            pltpu.make_async_remote_copy(
                src_ref=stat.at[s], dst_ref=got_stat.at[group, slot], send_sem=send_stat_sem,
                recv_sem=got_stat_sem.at[group], device_id={"sp": owner}, device_id_type=MESH).start()

    def combine(group):
        s = group * n + me
        pltpu.make_async_copy(got.at[group], got.at[group], got_sem.at[group]).wait()
        pltpu.make_async_copy(got_stat.at[group], got_stat.at[group], got_stat_sem.at[group]).wait()
        stats = [stat[s]] + [got_stat[group, r] for r in range(n - 1)]
        high = functools.reduce(jnp.maximum, [x[:1] for x in stats])
        scales = [jnp.exp(x[:1] - high) for x in stats]
        total = functools.reduce(jnp.add, [w * x[1:] for w, x in zip(scales, stats)])
        rows = jnp.concatenate([w / total for w in scales], 0)
        columns = jnp.transpose(rows)[:heads]
        result = part[s] * columns[:, :1]
        for r in range(n - 1):
            result += got[group, r].astype(F32) * columns[:, r + 1:r + 2]
        out[s] = result.astype(BF16)
        for r in range(1, n):
            pltpu.make_async_remote_copy(
                src_ref=out.at[s], dst_ref=out.at[s], send_sem=send_sem, recv_sem=out_sem,
                device_id={"sp": peer(r)}, device_id_type=MESH).start()

    q_copy.wait()
    k_copy(0).wait()
    pl.semaphore_wait(barrier, n - 1)

    def step(s, scores):
        k_copy(s).wait()
        v_copy(s - 1).wait()
        later = s + AHEAD - 1

        @pl.when(later < batch)
        def _():
            k_copy(later).start()
            v_copy(later).start()

        @pl.when(s >= 2)
        def _():
            send(s - 2)

        @pl.when((lax.rem(s, n) == n - 1) & (s >= 2 * n - 1))
        def _():
            combine(s // n - 1)

        new = scores_of(s)
        finish(s - 1, scores)
        return new

    scores = lax.fori_loop(1, batch, step, scores_of(0))
    v_copy(batch - 1).wait()
    finish(batch - 1, scores)
    send(batch - 2)
    send(batch - 1)
    combine(groups - 1)
    others = batch - groups
    pltpu.make_async_copy(out.at[pl.ds(0, others)], out.at[pl.ds(0, others)], out_sem).wait()
    o_ref[...] = out[...]
    pltpu.make_async_copy(out.at[pl.ds(0, others)], out.at[pl.ds(0, others)], send_sem).wait()
    pltpu.make_async_copy(out.at[pl.ds(0, others)], out.at[pl.ds(0, others)], send_sem).wait()
    pltpu.make_async_copy(stat.at[pl.ds(0, others)], stat.at[pl.ds(0, others)], send_stat_sem).wait()


def solution(mesh):
    n = mesh.shape["sp"]

    def step(q, k, v):
        batch, heads, head = q.shape
        tokens = k.shape[1]
        k = k.reshape(batch, tokens, head)
        v = v.reshape(batch, tokens, head)
        groups = batch // n
        return pl.pallas_call(
            functools.partial(kernel, n, head ** -0.5),
            out_shape=jax.ShapeDtypeStruct(q.shape, BF16),
            in_specs=[pl.BlockSpec(memory_space=pltpu.HBM)] * 3,
            out_specs=pl.BlockSpec(memory_space=pltpu.VMEM),
            scratch_shapes=[
                pltpu.VMEM((batch, heads, head), BF16),
                pltpu.VMEM((batch, tokens, head), BF16),
                pltpu.VMEM((batch, tokens, head), BF16),
                pltpu.VMEM((batch, heads, head), F32),
                pltpu.VMEM((batch, heads, head), BF16),
                pltpu.VMEM((batch, 2, 128), F32),
                pltpu.VMEM((groups, n - 1, heads, head), BF16),
                pltpu.VMEM((groups, n - 1, 2, 128), F32),
                pltpu.VMEM((batch, heads, head), BF16),
                pltpu.SemaphoreType.DMA,
                pltpu.SemaphoreType.DMA((batch,)),
                pltpu.SemaphoreType.DMA((batch,)),
                pltpu.SemaphoreType.DMA,
                pltpu.SemaphoreType.DMA,
                pltpu.SemaphoreType.DMA((groups,)),
                pltpu.SemaphoreType.DMA((groups,)),
                pltpu.SemaphoreType.DMA,
            ],
            compiler_params=pltpu.CompilerParams(
                collective_id=0, has_side_effects=True, vmem_limit_bytes=48 * 1024 * 1024),
            name="decode",
        )(q, k, v)

    return jax.shard_map(
        step,
        mesh=mesh,
        in_specs=(P("dp", None, None), P("dp", "sp", None, None), P("dp", "sp", None, None)),
        out_specs=P("dp", None, None),
        check_vma=False,
    )
```

time: 89.2 us -> 26.5 us (0.30)
  waiting for transfers between devices: 42.5 us -> 0 us
  Pallas kernels: 0 us -> 24.7 us
  matrix products: 18.4 us -> 0 us
  between operations: 13.4 us -> 0.01 us
  other arithmetic: 9.56 us -> 0 us
  local copies, waits for them, and re-layouts: 5.08 us -> 1.65 us
    all_gather x1 -> x0, waiting for transfers between devices: 42.5 us -> none  [step(): return together(lax.all_gather(part_of(q, k, v), 'sp')).reshape(q.shape)]
    pallas_call x0 -> x1, Pallas kernels: none -> 24.7 us  [step(): pl.pallas_call(functools.partial(kernel, n, head ** (-0.5)), out_shape=ja...]
    dot_general x2 -> x0, matrix products: 18.4 us -> none  [einsum(): return jnp.einsum(form, a.astype(jnp.float32), b.astype(jnp.float32))]
    slice x1 -> x0, other arithmetic: 4.43 us -> none  [together(): seen, total, high = (parts[..., :-2], parts[..., -2:-1], parts[..., -1:])]
    reduce_sum x3 -> x0, other arithmetic: 3.24 us -> none  [the longest x1 2.69 us: together(): jnp.sum(seen * scale, 0) / jnp.sum(total * scale, 0)]
    unnamed x5 -> x3, local copies, waits for them, and re-layouts: 4.38 us -> 1.65 us
    concatenate x1 -> x0, other arithmetic: 1.04 us -> none  [part_of(): jnp.concatenate([seen, jnp.sum(weights, -1, keepdims=True), high], -1)]
  transfers between devices with their start and end apart: 1 -> 0, of which waited for: 1 -> 0; matrix products, arithmetic and copies ran while one was open for 0% -> 0% of each run, Pallas kernels for 0% -> 0%
where the time goes in v1:
time: 26.5 us; the launch traced here: 26.3 us
  Pallas kernels  24.7 us (93%)
  local copies, waits for them, and re-layouts  1.65 us (6%)
    pallas_call x1, Pallas kernels, step(): pl.pallas_call(functools.partial(kernel, n, head ** (-0.5)), out_shape=ja...  24.7 us
    unnamed x3, local copies, waits for them, and re-layouts  1.65 us

profile of v1, /device:TPU:0, one launch (start us, length us, event | category | flops | bytes accessed | tf_op | source)
XLA Modules:
  0.0 26.3 jit_solution(1488769987001076978)
XLA Ops:
  0.0 0.0 copy-start
  0.0 0.9 %copy-done = bf16[32,16,256]{2,1,0:T(8,128)(2,1)S(1)} copy-done((bf16[32,16,256]{2,1,0:T(8,128)(2,1)S(1)}, bf16[32,16,256]{2,1,0:T(8,128)(2,1)}, u32[]{:S(2)}) %copy-start) | copy-done | bytes 262168
  1.0 24.7 %decode.1 = bf16[32,16,256]{2,1,0:T(8,128)(2,1)S(1)} custom-call(bf16[32,16,256]{2,1,0:T(8,128)(2,1)S(1)} %copy-done, bf16[32,1024,256]{2,1,0:T(8,128)(2,1)} %bitcast.2, bf16[32,1024,256]{2,1,0:T(8,128)(2,1)} %bitcast.3), custom_call_target="tpu_custom_call" | custom-call | tf_op jit(solution)/shard_map/decode/pallas_call | solution.py:139
  25.6 0.7 %copy.5 = bf16[32,16,256]{2,1,0:T(8,128)(2,1)} copy(bf16[32,16,256]{2,1,0:T(8,128)(2,1)S(1)} %decode.1) | data formatting | bytes 524288
Async XLA Ops:
  0.0 0.9 %copy-start = (bf16[32,16,256]{2,1,0:T(8,128)(2,1)S(1)}, bf16[32,16,256]{2,1,0:T(8,128)(2,1)}, u32[]{:S(2)}) copy-start(bf16[32,16,256]{2,1,0:T(8,128)(2,1)} %q_hbm.1) | copy-start | bytes 786436

commit v2 on v1

--- a/solution.py
+++ b/solution.py
@@ -10,40 +10,45 @@
 MESH = pl.DeviceIdType.MESH
 F32 = jnp.float32
 BF16 = jnp.bfloat16
-AHEAD = 4
+BLOCK = 2
+AHEAD = 2
 
 
-def kernel(n, scale, q_hbm, k_hbm, v_hbm, o_ref, q_buf, k_buf, v_buf, part, sent, stat, got, got_stat, out,
+def kernel(n, scale, q_hbm, k_hbm, v_hbm, o_ref, q_buf, k_buf, v_buf, raw, part, sent, stat, got, got_stat, out,
            q_sem, k_sem, v_sem, send_sem, send_stat_sem, got_sem, got_stat_sem, out_sem):
     me = lax.axis_index("sp")
     batch, heads, head = q_buf.shape
     groups = batch // n
+    blocks = batch // BLOCK
 
     def peer(r):
         return lax.rem(me + r, n)
 
-    def k_copy(s):
-        return pltpu.make_async_copy(k_hbm.at[s], k_buf.at[s], k_sem.at[s])
+    def k_copy(b):
+        run = pl.ds(b * BLOCK, BLOCK)
+        return pltpu.make_async_copy(k_hbm.at[run], k_buf.at[run], k_sem.at[lax.rem(b, 2 * AHEAD)])
 
-    def v_copy(s):
-        return pltpu.make_async_copy(v_hbm.at[s], v_buf.at[s], v_sem.at[s])
+    def v_copy(b):
+        run = pl.ds(b * BLOCK, BLOCK)
+        return pltpu.make_async_copy(v_hbm.at[run], v_buf.at[run], v_sem.at[lax.rem(b, 2 * AHEAD)])
 
     q_copy = pltpu.make_async_copy(q_hbm, q_buf, q_sem)
     k_copy(0).start()
     q_copy.start()
-    for s in range(AHEAD):
-        if s > 0:
-            k_copy(s).start()
-        v_copy(s).start()
+    for b in range(AHEAD):
+        if b > 0:
+            k_copy(b).start()
+        v_copy(b).start()
 
     barrier = pltpu.get_barrier_semaphore()
     for r in range(1, n):
         pl.semaphore_signal(barrier, inc=1, device_id={"sp": peer(r)}, device_id_type=MESH)
 
-    def scores_of(s):
-        return lax.dot_general(q_buf[s], k_buf[s], (((1,), (1,)), ((), ())), preferred_element_type=F32)
+    def scores_of(s, parity, j):
+        raw[parity][j] = lax.dot_general(q_buf[s], k_buf[s], (((1,), (1,)), ((), ())), preferred_element_type=F32)
 
-    def finish(s, scores):
+    def finish(s, parity, j):
+        scores = raw[parity][j]
         high = jnp.max(scores, -1, keepdims=True)
         weights = jnp.exp((scores - high) * scale)
         total = jnp.sum(weights, -1, keepdims=True)
@@ -90,35 +95,49 @@
     q_copy.wait()
     k_copy(0).wait()
     pl.semaphore_wait(barrier, n - 1)
+    for j in range(BLOCK):
+        scores_of(j, 0, j)
 
-    def step(s, scores):
-        k_copy(s).wait()
-        v_copy(s - 1).wait()
-        later = s + AHEAD - 1
+    def block(b, parity):
+        k_copy(b).wait()
+        v_copy(b - 1).wait()
+        later = b + AHEAD - 1
 
-        @pl.when(later < batch)
+        @pl.when(later < blocks)
         def _():
             k_copy(later).start()
             v_copy(later).start()
 
-        @pl.when(s >= 2)
+        @pl.when(b >= 2)
         def _():
-            send(s - 2)
+            for j in range(BLOCK):
+                send((b - 2) * BLOCK + j)
 
-        @pl.when((lax.rem(s, n) == n - 1) & (s >= 2 * n - 1))
+        for j in range(BLOCK):
+            scores_of(b * BLOCK + j, parity, j)
+        for j in range(BLOCK):
+            finish((b - 1) * BLOCK + j, 1 - parity, j)
+
+    per = n // BLOCK
+
+    def pair(i, _):
+        block(2 * i - 1, 1)
+        block(2 * i, 0)
+
+        @pl.when((lax.rem(2 * i, per) == 0) & (2 * i >= 2 * per))
         def _():
-            combine(s // n - 1)
+            combine(2 * i // per - 2)
+        return 0
 
-        new = scores_of(s)
-        finish(s - 1, scores)
-        return new
-
-    scores = lax.fori_loop(1, batch, step, scores_of(0))
-    v_copy(batch - 1).wait()
-    finish(batch - 1, scores)
-    send(batch - 2)
-    send(batch - 1)
-    combine(groups - 1)
+    lax.fori_loop(1, blocks // 2, pair, 0)
+    block(blocks - 1, 1)
+    v_copy(blocks - 1).wait()
+    for j in range(BLOCK):
+        finish((blocks - 1) * BLOCK + j, 1, j)
+    for j in range(2 * BLOCK):
+        send((blocks - 2) * BLOCK + j)
+    for group in range(groups - 2, groups):
+        combine(group)
     others = batch - groups
     pltpu.make_async_copy(out.at[pl.ds(0, others)], out.at[pl.ds(0, others)], out_sem).wait()
     o_ref[...] = out[...]
@@ -145,6 +164,7 @@
                 pltpu.VMEM((batch, heads, head), BF16),
                 pltpu.VMEM((batch, tokens, head), BF16),
                 pltpu.VMEM((batch, tokens, head), BF16),
+                [pltpu.VMEM((BLOCK, heads, tokens), F32)] * 2,
                 pltpu.VMEM((batch, heads, head), F32),
                 pltpu.VMEM((batch, heads, head), BF16),
                 pltpu.VMEM((batch, 2, 128), F32),
@@ -152,8 +172,8 @@
                 pltpu.VMEM((groups, n - 1, 2, 128), F32),
                 pltpu.VMEM((batch, heads, head), BF16),
                 pltpu.SemaphoreType.DMA,
-                pltpu.SemaphoreType.DMA((batch,)),
-                pltpu.SemaphoreType.DMA((batch,)),
+                pltpu.SemaphoreType.DMA((2 * AHEAD,)),
+                pltpu.SemaphoreType.DMA((2 * AHEAD,)),
                 pltpu.SemaphoreType.DMA,
                 pltpu.SemaphoreType.DMA,
                 pltpu.SemaphoreType.DMA((groups,)),
@@ -161,7 +181,7 @@
                 pltpu.SemaphoreType.DMA,
             ],
             compiler_params=pltpu.CompilerParams(
-                collective_id=0, has_side_effects=True, vmem_limit_bytes=48 * 1024 * 1024),
+                collective_id=0, has_side_effects=True, vmem_limit_bytes=67043328 - 320 * 1024),
             name="decode",
         )(q, k, v)
 

time: 26.5 us -> 33.4 us (1.26)
  Pallas kernels: 24.7 us -> 31.4 us
    pallas_call x1, Pallas kernels: 24.7 us -> 31.4 us  [step(): pl.pallas_call(functools.partial(kernel, n, head ** (-0.5)), out_shape=ja...]
    unnamed x3 -> x1, local copies, waits for them, and re-layouts: 1.65 us -> 1.67 us
where the time goes in v2:
time: 33.4 us; the launch traced here: 33 us
  Pallas kernels  31.4 us (94%)
  local copies, waits for them, and re-layouts  1.67 us (5%)
    pallas_call x1, Pallas kernels, step(): pl.pallas_call(functools.partial(kernel, n, head ** (-0.5)), out_shape=ja...  31.4 us
    unnamed x1, local copies, waits for them, and re-layouts  1.67 us

profile of v2, /device:TPU:0, one launch (start us, length us, event | category | flops | bytes accessed | tf_op | source)
XLA Modules:
  0.0 33.0 jit_solution(16599374197576300114)
XLA Ops:
  0.0 31.4 %decode.1 = bf16[32,16,256]{2,1,0:T(8,128)(2,1)} custom-call(bf16[32,16,256]{2,1,0:T(8,128)(2,1)} %q_hbm.1, bf16[32,1024,256]{2,1,0:T(8,128)(2,1)} %bitcast.2, bf16[32,1024,256]{2,1,0:T(8,128)(2,1)} %bitcast.3), custom_call_target="tpu_custom_call" | custom-call | tf_op jit(solution)/shard_map/decode/pallas_call | solution.py:158
  31.4 1.7 %copy.5 = bf16[32,16,256]{2,1,0:T(8,128)(2,1)} copy(bf16[32,16,256]{2,1,0:T(8,128)(2,1)} %decode.1) | data formatting | bytes 524288

commit v3 on v2

--- a/solution.py
+++ b/solution.py
@@ -11,7 +11,8 @@
 F32 = jnp.float32
 BF16 = jnp.bfloat16
 BLOCK = 2
-AHEAD = 2
+PIECES = 2
+AHEAD = 3
 
 
 def kernel(n, scale, q_hbm, k_hbm, v_hbm, o_ref, q_buf, k_buf, v_buf, raw, part, sent, stat, got, got_stat, out,
@@ -24,13 +25,23 @@
     def peer(r):
         return lax.rem(me + r, n)
 
-    def k_copy(b):
-        run = pl.ds(b * BLOCK, BLOCK)
-        return pltpu.make_async_copy(k_hbm.at[run], k_buf.at[run], k_sem.at[lax.rem(b, 2 * AHEAD)])
-
-    def v_copy(b):
-        run = pl.ds(b * BLOCK, BLOCK)
-        return pltpu.make_async_copy(v_hbm.at[run], v_buf.at[run], v_sem.at[lax.rem(b, 2 * AHEAD)])
+    class Run:
+        def __init__(self, hbm, buf, sem, b):
+            self.hbm, self.buf, self.first, self.sem = hbm, buf, b * BLOCK, sem.at[lax.rem(b, 2 * AHEAD)]
+
+        def start(self):
+            rows = k_buf.shape[1] // PIECES
+            for j in range(BLOCK):
+                for p in range(PIECES):
+                    at = (self.first + j, pl.ds(p * rows, rows))
+                    pltpu.make_async_copy(self.hbm.at[at], self.buf.at[at], self.sem).start()
+
+        def wait(self):
+            run = self.buf.at[pl.ds(self.first, BLOCK)]
+            pltpu.make_async_copy(run, run, self.sem).wait()
+
+    k_copy = functools.partial(Run, k_hbm, k_buf, k_sem)
+    v_copy = functools.partial(Run, v_hbm, v_buf, v_sem)
 
     q_copy = pltpu.make_async_copy(q_hbm, q_buf, q_sem)
     k_copy(0).start()
@@ -181,9 +192,9 @@
                 pltpu.SemaphoreType.DMA,
             ],
             compiler_params=pltpu.CompilerParams(
-                collective_id=0, has_side_effects=True, vmem_limit_bytes=67043328 - 320 * 1024),
+                collective_id=0, has_side_effects=True, vmem_limit_bytes=48 * 1024 * 1024),
             name="decode",
-        )(q, k, v)
+        )(pltpu.with_memory_space_constraint(q, pltpu.HBM), k, v)
 
     return jax.shard_map(
         step,

time: 33.4 us -> 24.7 us (0.74)
  Pallas kernels: 31.4 us -> 23.8 us
  local copies, waits for them, and re-layouts: 1.67 us -> 0.71 us
    pallas_call x1, Pallas kernels: 31.4 us -> 23.8 us  [step(): pl.pallas_call(functools.partial(kernel, n, head ** (-0.5)), out_shape=ja...]
    unnamed x1, local copies, waits for them, and re-layouts: 1.67 us -> 0.71 us
where the time goes in v3:
time: 24.7 us; the launch traced here: 24.5 us
  Pallas kernels  23.8 us (96%)
  local copies, waits for them, and re-layouts  0.71 us (3%)
    pallas_call x1, Pallas kernels, step(): pl.pallas_call(functools.partial(kernel, n, head ** (-0.5)), out_shape=ja...  23.8 us
    unnamed x1, local copies, waits for them, and re-layouts  0.71 us

profile of v3, /device:TPU:0, one launch (start us, length us, event | category | flops | bytes accessed | tf_op | source)
XLA Modules:
  0.0 24.5 jit_solution(6026658334143828860)
XLA Ops:
  0.0 23.8 %decode.1 = bf16[32,16,256]{2,1,0:T(8,128)(2,1)S(1)} custom-call(bf16[32,16,256]{2,1,0:T(8,128)(2,1)} %q_hbm.1, bf16[32,1024,256]{2,1,0:T(8,128)(2,1)} %bitcast.2, bf16[32,1024,256]{2,1,0:T(8,128)(2,1)} %bitcast.3), custom_call_target="tpu_custom_call" | custom-call | tf_op jit(solution)/shard_map/decode/pallas_call | solution.py:169
  23.8 0.7 %copy.5 = bf16[32,16,256]{2,1,0:T(8,128)(2,1)} copy(bf16[32,16,256]{2,1,0:T(8,128)(2,1)S(1)} %decode.1) | data formatting | bytes 524288

commit v4 on v3

--- a/solution.py
+++ b/solution.py
@@ -12,7 +12,7 @@
 BF16 = jnp.bfloat16
 BLOCK = 2
 PIECES = 2
-AHEAD = 3
+AHEAD = 5
 
 
 def kernel(n, scale, q_hbm, k_hbm, v_hbm, o_ref, q_buf, k_buf, v_buf, raw, part, sent, stat, got, got_stat, out,

time: 24.7 us -> 24.2 us (0.980)
  Pallas kernels: 23.8 us -> 23.4 us
    pallas_call x1, Pallas kernels: 23.8 us -> 23.4 us  [step(): pl.pallas_call(functools.partial(kernel, n, head ** (-0.5)), out_shape=ja...]
where the time goes in v4:
time: 24.2 us; the launch traced here: 24.1 us
  Pallas kernels  23.4 us (97%)
  local copies, waits for them, and re-layouts  0.71 us (3%)
    pallas_call x1, Pallas kernels, step(): pl.pallas_call(functools.partial(kernel, n, head ** (-0.5)), out_shape=ja...  23.4 us
    unnamed x1, local copies, waits for them, and re-layouts  0.71 us

profile of v4, /device:TPU:0, one launch (start us, length us, event | category | flops | bytes accessed | tf_op | source)
XLA Modules:
  0.0 24.1 jit_solution(14491389560878604256)
XLA Ops:
  0.0 23.4 %decode.1 = bf16[32,16,256]{2,1,0:T(8,128)(2,1)S(1)} custom-call(bf16[32,16,256]{2,1,0:T(8,128)(2,1)} %q_hbm.1, bf16[32,1024,256]{2,1,0:T(8,128)(2,1)} %bitcast.2, bf16[32,1024,256]{2,1,0:T(8,128)(2,1)} %bitcast.3), custom_call_target="tpu_custom_call" | custom-call | tf_op jit(solution)/shard_map/decode/pallas_call | solution.py:169
  23.4 0.7 %copy.5 = bf16[32,16,256]{2,1,0:T(8,128)(2,1)} copy(bf16[32,16,256]{2,1,0:T(8,128)(2,1)S(1)} %decode.1) | data formatting | bytes 524288

commit v5 on v0

v5 whole, which is shorter than its diff:
```python
import functools

import jax
import jax.numpy as jnp
from jax import lax
from jax.experimental import pallas as pl
from jax.experimental.pallas import tpu as pltpu
from jax.sharding import PartitionSpec as P

MESH = pl.DeviceIdType.MESH
F32 = jnp.float32
BF16 = jnp.bfloat16
BLOCK = 2
PIECES = 2
AHEAD = 5
DIRECT = 3
CUTS = (0, 6, 10)
LANES = 128


def kernel(n, scale, q_hbm, k_hbm, v_hbm, o_ref, q_buf, k_buf, v_buf, raw0, raw1, part, other, mine, mine_stat, theirs,
           theirs_stat, out, q_sem, k_sem, v_sem, pair_send, pair_recv, acc_send, stat_send, acc_recv, stat_recv,
           direct_acc_recv, direct_stat_recv, direct_acc_recv2, direct_stat_recv2, out_send, out_recv):
    me = lax.axis_index("sp")
    chip, core = me // 2, lax.rem(me, 2)
    chips = n // 2
    batch, heads, head = q_buf.shape
    tokens = k_buf.shape[1]
    blocks = batch // BLOCK
    staged = blocks - DIRECT
    groups = list(zip(CUTS, CUTS[1:] + (staged,)))
    raw = (raw0, raw1)

    def device(r, same):
        return lax.rem(chip + r, chips) * 2 + (core if same else 1 - core)

    class Run:
        def __init__(self, hbm, buf, sem, b):
            self.hbm, self.buf, self.first, self.sem = hbm, buf, b * BLOCK, sem.at[lax.rem(b, 2 * AHEAD)]

        def start(self):
            rows = tokens // PIECES
            for j in range(BLOCK):
                for p in range(PIECES):
                    at = (self.first + j, pl.ds(p * rows, rows))
                    pltpu.make_async_copy(self.hbm.at[at], self.buf.at[at], self.sem).start()

        def wait(self):
            run = self.buf.at[pl.ds(self.first, BLOCK)]
            pltpu.make_async_copy(run, run, self.sem).wait()

    k_copy = functools.partial(Run, k_hbm, k_buf, k_sem)
    v_copy = functools.partial(Run, v_hbm, v_buf, v_sem)

    def wait(ref, sem):
        pltpu.make_async_copy(ref, ref, sem).wait()

    def remote(src, dst, send_sem, recv_sem, to):
        pltpu.make_async_remote_copy(src_ref=src, dst_ref=dst, send_sem=send_sem, recv_sem=recv_sem,
                                     device_id={"sp": to}, device_id_type=MESH).start()

    q_copy = pltpu.make_async_copy(q_hbm, q_buf, q_sem)
    k_copy(0).start()
    q_copy.start()
    for b in range(AHEAD):
        if b > 0:
            k_copy(b).start()
        v_copy(b).start()

    barrier = pltpu.get_barrier_semaphore()
    for r in range(1, n):
        pl.semaphore_signal(barrier, inc=1, device_id={"sp": lax.rem(me + r, n)}, device_id_type=MESH)

    lane = lax.broadcasted_iota(jnp.int32, (heads, LANES), 1)

    def scores_of(s, to):
        to[...] = lax.dot_general(q_buf[s], k_buf[s], (((1,), (1,)), ((), ())), preferred_element_type=F32)

    def finish(s, raw):
        scores = raw[...]
        high = jnp.max(scores, -1, keepdims=True)
        weights = jnp.exp((scores - high) * scale)
        total = jnp.sum(weights, -1, keepdims=True)
        part[s, :, :head] = jnp.dot(weights.astype(BF16), v_buf[s], preferred_element_type=F32)
        part[s, :, head:] = jnp.where(lane == 0, high * scale, total)

    def to_pair(t):
        remote(part.at[BLOCK * t + 1 - core], other.at[t], pair_send, pair_recv.at[lax.rem(t, 8)], device(0, False))

    def add_pair(t):
        a, b = part[BLOCK * t + core], other[t]
        high_a, high_b = a[:, head:head + 1], b[:, head:head + 1]
        high = jnp.maximum(high_a, high_b)
        scale_a, scale_b = jnp.exp(high_a - high), jnp.exp(high_b - high)
        total = scale_a * a[:, head + 1:head + 2] + scale_b * b[:, head + 1:head + 2]
        mine[t, chip] = (scale_a * a[:, :head] + scale_b * b[:, :head]).astype(BF16)
        mine_stat[t, chip, :, :heads] = jnp.transpose(jnp.where(lane == 0, high, total))[:2]

    def group_of(t):
        return sum((t >= cut).astype(jnp.int32) if not isinstance(t, int) else int(t >= cut) for cut in CUTS[1:])

    def to_chips(t):
        group = group_of(t)
        for r in range(1, chips):
            remote(mine.at[t, chip], mine.at[t, chip], acc_send, acc_recv.at[group], device(r, True))
            remote(mine_stat.at[t, chip], mine_stat.at[t, chip], stat_send, stat_recv.at[group], device(r, True))

    def to_all(t):
        d = t - staged
        for r in range(chips):
            if r > 0:
                remote(mine.at[t, chip], mine.at[t, chip], acc_send, direct_acc_recv.at[d], device(r, True))
                remote(mine_stat.at[t, chip], mine_stat.at[t, chip], stat_send, direct_stat_recv.at[d], device(r, True))
            remote(mine.at[t, chip], theirs.at[d, chip], acc_send, direct_acc_recv2.at[d], device(r, False))
            remote(mine_stat.at[t, chip], theirs_stat.at[d, chip], stat_send, direct_stat_recv2.at[d], device(r, False))

    def add_chips(work):
        rows = []
        for _, stat, _, _ in work:
            highs = [stat[c, 0:1] for c in range(chips)]
            totals = [stat[c, 1:2] for c in range(chips)]
            high = functools.reduce(jnp.maximum, highs)
            scales = [jnp.exp(x - high) for x in highs]
            total = functools.reduce(jnp.add, [w * x for w, x in zip(scales, totals)])
            rows += [w / total for w in scales]
        while len(rows) % 8:
            rows.append(rows[-1])
        columns = jnp.transpose(jnp.concatenate(rows, 0))[:heads]
        for i, (acc, _, t, j) in enumerate(work):
            terms = [acc[c].astype(F32) * columns[:, i * chips + c:i * chips + c + 1] for c in range(chips)]
            out[t, j] = functools.reduce(jnp.add, terms).astype(BF16)

    def add_group(g):
        first, last = groups[g]
        count = (last - first) * (chips - 1)
        flat = mine.at[pl.ds(0, count // (chips - 1)), pl.ds(0, chips - 1)]
        flat_stat = mine_stat.at[pl.ds(0, count // (chips - 1)), pl.ds(0, chips - 1)]
        wait(flat, acc_recv.at[g])
        wait(flat_stat, stat_recv.at[g])
        add_chips([(mine.at[t], mine_stat.at[t], t, core) for t in range(first, last)])
        run = pl.ds(first, last - first)
        remote(out.at[run, core], out.at[run, core], out_send, out_recv, device(0, False))

    def block(b):
        b, parity, first, last = b if isinstance(b, tuple) else (b, b % 2, b, b)
        if first < blocks:
            k_copy(b).wait()
        v_copy(b - 1).wait()
        if first >= 4:
            wait(other.at[0], pair_recv.at[lax.rem(b - 4, 8)])
        if first < blocks:
            later = b + AHEAD - 1
            if last + AHEAD - 1 < blocks:
                k_copy(later).start()
                v_copy(later).start()
            elif first + AHEAD - 1 < blocks:
                @pl.when(later < blocks)
                def _():
                    k_copy(later).start()
                    v_copy(later).start()
        if first == 2:
            pl.semaphore_wait(barrier, n - 1)
        if first >= 2:
            to_pair(b - 2)
        if first >= 5:
            to_chips(b - 5)
        if first < blocks:
            for j in range(BLOCK):
                scores_of(b * BLOCK + j, raw[parity].at[j])
        for j in range(BLOCK):
            finish((b - 1) * BLOCK + j, raw[1 - parity].at[j])
        if first >= 4:
            add_pair(b - 4)

    q_copy.wait()
    k_copy(0).wait()
    for j in range(BLOCK):
        scores_of(j, raw[0].at[j])
    for b in range(1, 5):
        block(b)

    def two(i, _):
        block((2 * i + 5, 1, 5, blocks - 2))
        block((2 * i + 6, 0, 5, blocks - 2))
        return 0

    lax.fori_loop(0, (blocks - 6) // 2, two, 0)
    block(blocks - 1)
    block(blocks)
    to_pair(blocks - 1)
    to_chips(blocks - 4)
    for t in range(blocks - 3, blocks):
        if t == blocks - 1:
            add_group(0)
        wait(other.at[0], pair_recv.at[t % 8])
        add_pair(t)
        to_all(t)
    for g in range(1, len(groups)):
        add_group(g)
    for d in range(DIRECT):
        wait(mine.at[0, pl.ds(0, chips - 1)], direct_acc_recv.at[d])
        wait(mine_stat.at[0, pl.ds(0, chips - 1)], direct_stat_recv.at[d])
        wait(mine.at[0], direct_acc_recv2.at[d])
        wait(mine_stat.at[0], direct_stat_recv2.at[d])
        t = staged + d
        add_chips([(mine.at[t], mine_stat.at[t], t, core), (theirs.at[d], theirs_stat.at[d], t, 1 - core)])
    wait(out.at[pl.ds(0, staged), 0], out_recv)
    for t in range(blocks):
        for j in range(BLOCK):
            o_ref[t * BLOCK + j] = out[t, j]
    wait(out.at[pl.ds(0, staged), 0], out_send)
    wait(part.at[pl.ds(0, blocks)], pair_send)
    sends = (staged * (chips - 1) + DIRECT * (n - 1)) // chips
    wait(mine.at[pl.ds(0, sends)], acc_send)
    wait(mine_stat.at[pl.ds(0, sends)], stat_send)


def solution(mesh):
    n = mesh.shape["sp"]

    def step(q, k, v):
        batch, heads, head = q.shape
        tokens = k.shape[1]
        k = k.reshape(batch, tokens, head)
        v = v.reshape(batch, tokens, head)
        blocks, chips = batch // BLOCK, n // 2
        dma = pltpu.SemaphoreType.DMA
        return pl.pallas_call(
            functools.partial(kernel, n, head ** -0.5),
            out_shape=jax.ShapeDtypeStruct(q.shape, BF16),
            in_specs=[pl.BlockSpec(memory_space=pltpu.HBM)] * 3,
            out_specs=pl.BlockSpec(memory_space=pltpu.VMEM),
            scratch_shapes=[
                pltpu.VMEM((batch, heads, head), BF16),
                pltpu.VMEM((batch, tokens, head), BF16),
                pltpu.VMEM((batch, tokens, head), BF16),
                pltpu.VMEM((BLOCK, heads, tokens), F32),
                pltpu.VMEM((BLOCK, heads, tokens), F32),
                pltpu.VMEM((batch, heads, head + LANES), F32),
                pltpu.VMEM((blocks, heads, head + LANES), F32),
                pltpu.VMEM((blocks, chips, heads, head), BF16),
                pltpu.VMEM((blocks, chips, 2, LANES), F32),
                pltpu.VMEM((DIRECT, chips, heads, head), BF16),
                pltpu.VMEM((DIRECT, chips, 2, LANES), F32),
                pltpu.VMEM((blocks, BLOCK, heads, head), BF16),
                dma, dma((2 * AHEAD,)), dma((2 * AHEAD,)),
                dma, dma((8,)),
                dma, dma, dma((len(CUTS),)), dma((len(CUTS),)),
                dma((DIRECT,)), dma((DIRECT,)), dma((DIRECT,)), dma((DIRECT,)),
                dma, dma,
            ],
            compiler_params=pltpu.CompilerParams(
                collective_id=0, has_side_effects=True, vmem_limit_bytes=48 * 1024 * 1024),
            name="decode",
        )(pltpu.with_memory_space_constraint(q, pltpu.HBM), k, v)

    return jax.shard_map(
        step,
        mesh=mesh,
        in_specs=(P("dp", None, None), P("dp", "sp", None, None), P("dp", "sp", None, None)),
        out_specs=P("dp", None, None),
        check_vma=False,
    )
```

time: 89.2 us -> 24.6 us (0.28)
  waiting for transfers between devices: 42.5 us -> 0 us
  Pallas kernels: 0 us -> 23.8 us
  matrix products: 18.4 us -> 0 us
  between operations: 13.4 us -> 0.01 us
  other arithmetic: 9.56 us -> 0 us
  local copies, waits for them, and re-layouts: 5.08 us -> 0.71 us
    all_gather x1 -> x0, waiting for transfers between devices: 42.5 us -> none  [step(): return together(lax.all_gather(part_of(q, k, v), 'sp')).reshape(q.shape)]
    pallas_call x0 -> x1, Pallas kernels: none -> 23.8 us  [step(): pl.pallas_call(functools.partial(kernel, n, head ** (-0.5)), out_shape=ja...]
    dot_general x2 -> x0, matrix products: 18.4 us -> none  [einsum(): return jnp.einsum(form, a.astype(jnp.float32), b.astype(jnp.float32))]
    slice x1 -> x0, other arithmetic: 4.43 us -> none  [together(): seen, total, high = (parts[..., :-2], parts[..., -2:-1], parts[..., -1:])]
    unnamed x5 -> x1, local copies, waits for them, and re-layouts: 4.38 us -> 0.71 us
    reduce_sum x3 -> x0, other arithmetic: 3.24 us -> none  [the longest x1 2.69 us: together(): jnp.sum(seen * scale, 0) / jnp.sum(total * scale, 0)]
    concatenate x1 -> x0, other arithmetic: 1.04 us -> none  [part_of(): jnp.concatenate([seen, jnp.sum(weights, -1, keepdims=True), high], -1)]
  transfers between devices with their start and end apart: 1 -> 0, of which waited for: 1 -> 0; matrix products, arithmetic and copies ran while one was open for 0% -> 0% of each run, Pallas kernels for 0% -> 0%
where the time goes in v5:
time: 24.6 us; the launch traced here: 24.5 us
  Pallas kernels  23.8 us (97%)
  local copies, waits for them, and re-layouts  0.71 us (3%)
    pallas_call x1, Pallas kernels, step(): pl.pallas_call(functools.partial(kernel, n, head ** (-0.5)), out_shape=ja...  23.8 us
    unnamed x1, local copies, waits for them, and re-layouts  0.71 us

profile of v5, /device:TPU:0, one launch (start us, length us, event | category | flops | bytes accessed | tf_op | source)
XLA Modules:
  0.0 24.5 jit_solution(10810820587798405625)
XLA Ops:
  0.0 23.8 %decode.1 = bf16[32,16,256]{2,1,0:T(8,128)(2,1)S(1)} custom-call(bf16[32,16,256]{2,1,0:T(8,128)(2,1)} %q_hbm.1, bf16[32,1024,256]{2,1,0:T(8,128)(2,1)} %bitcast.2, bf16[32,1024,256]{2,1,0:T(8,128)(2,1)} %bitcast.3), custom_call_target="tpu_custom_call" | custom-call | tf_op jit(solution)/shard_map/decode/pallas_call | solution.py:228
  23.8 0.7 %copy.5 = bf16[32,16,256]{2,1,0:T(8,128)(2,1)} copy(bf16[32,16,256]{2,1,0:T(8,128)(2,1)S(1)} %decode.1) | data formatting | bytes 524288

commit v6 on v5

--- a/solution.py
+++ b/solution.py
@@ -13,7 +13,7 @@
 BLOCK = 2
 PIECES = 2
 AHEAD = 5
-DIRECT = 3
+DIRECT = 1
 CUTS = (0, 6, 10)
 LANES = 128
 
@@ -194,7 +194,7 @@
             add_group(0)
         wait(other.at[0], pair_recv.at[t % 8])
         add_pair(t)
-        to_all(t)
+        (to_all if t >= staged else to_chips)(t)
     for g in range(1, len(groups)):
         add_group(g)
     for d in range(DIRECT):

time: 24.6 us -> 24 us (0.976)
  Pallas kernels: 23.8 us -> 23.2 us
    pallas_call x1, Pallas kernels: 23.8 us -> 23.2 us  [step(): pl.pallas_call(functools.partial(kernel, n, head ** (-0.5)), out_shape=ja...]
where the time goes in v6:
time: 24 us
  Pallas kernels  23.2 us (97%)
  local copies, waits for them, and re-layouts  0.71 us (3%)
    pallas_call x1, Pallas kernels, step(): pl.pallas_call(functools.partial(kernel, n, head ** (-0.5)), out_shape=ja...  23.2 us
    unnamed x1, local copies, waits for them, and re-layouts  0.71 us

profile of v6, /device:TPU:0, one launch (start us, length us, event | category | flops | bytes accessed | tf_op | source)
XLA Modules:
  0.0 24.0 jit_solution(13266195547613627953)
XLA Ops:
  0.0 23.2 %decode.1 = bf16[32,16,256]{2,1,0:T(8,128)(2,1)S(1)} custom-call(bf16[32,16,256]{2,1,0:T(8,128)(2,1)} %q_hbm.1, bf16[32,1024,256]{2,1,0:T(8,128)(2,1)} %bitcast.2, bf16[32,1024,256]{2,1,0:T(8,128)(2,1)} %bitcast.3), custom_call_target="tpu_custom_call" | custom-call | tf_op jit(solution)/shard_map/decode/pallas_call | solution.py:228
  23.2 0.7 %copy.5 = bf16[32,16,256]{2,1,0:T(8,128)(2,1)} copy(bf16[32,16,256]{2,1,0:T(8,128)(2,1)S(1)} %decode.1) | data formatting | bytes 524288

commit v7 on v6

--- a/solution.py
+++ b/solution.py
@@ -82,19 +82,23 @@
         weights = jnp.exp((scores - high) * scale)
         total = jnp.sum(weights, -1, keepdims=True)
         part[s, :, :head] = jnp.dot(weights.astype(BF16), v_buf[s], preferred_element_type=F32)
-        part[s, :, head:] = jnp.where(lane == 0, high * scale, total)
+        part[s, :, head:head + LANES] = jnp.broadcast_to(high * scale, (heads, LANES))
+        part[s, :, head + LANES:] = jnp.broadcast_to(total, (heads, LANES))
 
     def to_pair(t):
         remote(part.at[BLOCK * t + 1 - core], other.at[t], pair_send, pair_recv.at[lax.rem(t, 8)], device(0, False))
 
     def add_pair(t):
-        a, b = part[BLOCK * t + core], other[t]
-        high_a, high_b = a[:, head:head + 1], b[:, head:head + 1]
+        a, b = part.at[BLOCK * t + core], other.at[t]
+        high_a, high_b = a[:, head:head + LANES], b[:, head:head + LANES]
         high = jnp.maximum(high_a, high_b)
         scale_a, scale_b = jnp.exp(high_a - high), jnp.exp(high_b - high)
-        total = scale_a * a[:, head + 1:head + 2] + scale_b * b[:, head + 1:head + 2]
-        mine[t, chip] = (scale_a * a[:, :head] + scale_b * b[:, :head]).astype(BF16)
-        mine_stat[t, chip, :, :heads] = jnp.transpose(jnp.where(lane == 0, high, total))[:2]
+        total = scale_a * a[:, head + LANES:] + scale_b * b[:, head + LANES:]
+        for at in range(0, head, LANES):
+            run = slice(at, at + LANES)
+            mine[t, chip, :, run] = (scale_a * a[:, run] + scale_b * b[:, run]).astype(BF16)
+        both = jnp.where(lane == 0, high, total)
+        mine_stat[t, chip, :, :chips * heads] = jnp.transpose(jnp.concatenate([both] * chips, 0))[:2]
 
     def group_of(t):
         return sum((t >= cut).astype(jnp.int32) if not isinstance(t, int) else int(t >= cut) for cut in CUTS[1:])
@@ -114,21 +118,28 @@
             remote(mine.at[t, chip], theirs.at[d, chip], acc_send, direct_acc_recv2.at[d], device(r, False))
             remote(mine_stat.at[t, chip], theirs_stat.at[d, chip], stat_send, direct_stat_recv2.at[d], device(r, False))
 
+    wide = chips * heads
+    owner = lax.broadcasted_iota(jnp.int32, (1, wide), 1) // heads
+    diagonal = lax.rem(lax.broadcasted_iota(jnp.int32, (heads, wide), 1), heads) == lax.broadcasted_iota(
+        jnp.int32, (heads, wide), 0)
+
     def add_chips(work):
-        rows = []
-        for _, stat, _, _ in work:
-            highs = [stat[c, 0:1] for c in range(chips)]
-            totals = [stat[c, 1:2] for c in range(chips)]
+        for acc, stat, t, j in work:
+            highs = [stat[c, 0:1, :wide] for c in range(chips)]
+            totals = [stat[c, 1:2, :wide] for c in range(chips)]
             high = functools.reduce(jnp.maximum, highs)
             scales = [jnp.exp(x - high) for x in highs]
             total = functools.reduce(jnp.add, [w * x for w, x in zip(scales, totals)])
-            rows += [w / total for w in scales]
-        while len(rows) % 8:
-            rows.append(rows[-1])
-        columns = jnp.transpose(jnp.concatenate(rows, 0))[:heads]
-        for i, (acc, _, t, j) in enumerate(work):
-            terms = [acc[c].astype(F32) * columns[:, i * chips + c:i * chips + c + 1] for c in range(chips)]
-            out[t, j] = functools.reduce(jnp.add, terms).astype(BF16)
+            row = scales[0]
+            for c in range(1, chips):
+                row = jnp.where(owner == c, scales[c], row)
+            rest = jnp.where(diagonal, jnp.broadcast_to(row / total, (heads, wide)), 0.0)
+            terms = []
+            for _ in range(3):
+                terms.append(rest.astype(BF16))
+                rest = rest - terms[-1].astype(F32)
+            sums = jnp.dot(jnp.concatenate(terms, 0), acc[...].reshape(wide, head), preferred_element_type=F32)
+            out[t, j] = (sums[:heads] + (sums[heads:2 * heads] + sums[2 * heads:])).astype(BF16)
 
     def add_group(g):
         first, last = groups[g]
@@ -236,8 +247,8 @@
                 pltpu.VMEM((batch, tokens, head), BF16),
                 pltpu.VMEM((BLOCK, heads, tokens), F32),
                 pltpu.VMEM((BLOCK, heads, tokens), F32),
-                pltpu.VMEM((batch, heads, head + LANES), F32),
-                pltpu.VMEM((blocks, heads, head + LANES), F32),
+                pltpu.VMEM((batch, heads, head + 2 * LANES), F32),
+                pltpu.VMEM((blocks, heads, head + 2 * LANES), F32),
                 pltpu.VMEM((blocks, chips, heads, head), BF16),
                 pltpu.VMEM((blocks, chips, 2, LANES), F32),
                 pltpu.VMEM((DIRECT, chips, heads, head), BF16),

time: 24 us -> 23 us (0.958)
  Pallas kernels: 23.2 us -> 22.2 us
    pallas_call x1, Pallas kernels: 23.2 us -> 22.2 us  [step(): pl.pallas_call(functools.partial(kernel, n, head ** (-0.5)), out_shape=ja...]
where the time goes in v7:
time: 23 us; the launch traced here: 22.9 us
  Pallas kernels  22.2 us (97%)
  local copies, waits for them, and re-layouts  0.71 us (3%)
    pallas_call x1, Pallas kernels, step(): pl.pallas_call(functools.partial(kernel, n, head ** (-0.5)), out_shape=ja...  22.2 us
    unnamed x1, local copies, waits for them, and re-layouts  0.71 us

profile of v7, /device:TPU:0, one launch (start us, length us, event | category | flops | bytes accessed | tf_op | source)
XLA Modules:
  0.0 22.9 jit_solution(7665829565664392509)
XLA Ops:
  0.0 22.2 %decode.1 = bf16[32,16,256]{2,1,0:T(8,128)(2,1)S(1)} custom-call(bf16[32,16,256]{2,1,0:T(8,128)(2,1)} %q_hbm.1, bf16[32,1024,256]{2,1,0:T(8,128)(2,1)} %bitcast.2, bf16[32,1024,256]{2,1,0:T(8,128)(2,1)} %bitcast.3), custom_call_target="tpu_custom_call" | custom-call | tf_op jit(solution)/shard_map/decode/pallas_call | solution.py:239
  22.2 0.7 %copy.5 = bf16[32,16,256]{2,1,0:T(8,128)(2,1)} copy(bf16[32,16,256]{2,1,0:T(8,128)(2,1)S(1)} %decode.1) | data formatting | bytes 524288

commit v8 on v7

--- a/solution.py
+++ b/solution.py
@@ -14,6 +14,7 @@
 PIECES = 2
 AHEAD = 5
 DIRECT = 1
+LAG = 6
 CUTS = (0, 6, 10)
 LANES = 128
 
@@ -86,7 +87,7 @@
         part[s, :, head + LANES:] = jnp.broadcast_to(total, (heads, LANES))
 
     def to_pair(t):
-        remote(part.at[BLOCK * t + 1 - core], other.at[t], pair_send, pair_recv.at[lax.rem(t, 8)], device(0, False))
+        remote(part.at[BLOCK * t + 1 - core], other.at[t], pair_send, pair_recv.at[t], device(0, False))
 
     def add_pair(t):
         a, b = part.at[BLOCK * t + core], other.at[t]
@@ -157,8 +158,8 @@
         if first < blocks:
             k_copy(b).wait()
         v_copy(b - 1).wait()
-        if first >= 4:
-            wait(other.at[0], pair_recv.at[lax.rem(b - 4, 8)])
+        if first >= LAG:
+            wait(other.at[0], pair_recv.at[b - LAG])
         if first < blocks:
             later = b + AHEAD - 1
             if last + AHEAD - 1 < blocks:
@@ -173,37 +174,37 @@
             pl.semaphore_wait(barrier, n - 1)
         if first >= 2:
             to_pair(b - 2)
-        if first >= 5:
-            to_chips(b - 5)
+        if first > LAG:
+            to_chips(b - LAG - 1)
         if first < blocks:
             for j in range(BLOCK):
                 scores_of(b * BLOCK + j, raw[parity].at[j])
         for j in range(BLOCK):
             finish((b - 1) * BLOCK + j, raw[1 - parity].at[j])
-        if first >= 4:
-            add_pair(b - 4)
+        if first >= LAG:
+            add_pair(b - LAG)
 
     q_copy.wait()
     k_copy(0).wait()
     for j in range(BLOCK):
         scores_of(j, raw[0].at[j])
-    for b in range(1, 5):
+    for b in range(1, LAG + 1):
         block(b)
 
     def two(i, _):
-        block((2 * i + 5, 1, 5, blocks - 2))
-        block((2 * i + 6, 0, 5, blocks - 2))
+        block((2 * i + LAG + 1, 1, LAG + 1, blocks - 2))
+        block((2 * i + LAG + 2, 0, LAG + 1, blocks - 2))
         return 0
 
-    lax.fori_loop(0, (blocks - 6) // 2, two, 0)
+    lax.fori_loop(0, (blocks - LAG - 2) // 2, two, 0)
     block(blocks - 1)
     block(blocks)
     to_pair(blocks - 1)
-    to_chips(blocks - 4)
-    for t in range(blocks - 3, blocks):
+    to_chips(blocks - LAG)
+    for t in range(blocks - LAG + 1, blocks):
         if t == blocks - 1:
             add_group(0)
-        wait(other.at[0], pair_recv.at[t % 8])
+        wait(other.at[0], pair_recv.at[t])
         add_pair(t)
         (to_all if t >= staged else to_chips)(t)
     for g in range(1, len(groups)):
@@ -255,7 +256,7 @@
                 pltpu.VMEM((DIRECT, chips, 2, LANES), F32),
                 pltpu.VMEM((blocks, BLOCK, heads, head), BF16),
                 dma, dma((2 * AHEAD,)), dma((2 * AHEAD,)),
-                dma, dma((8,)),
+                dma, dma((blocks,)),
                 dma, dma, dma((len(CUTS),)), dma((len(CUTS),)),
                 dma((DIRECT,)), dma((DIRECT,)), dma((DIRECT,)), dma((DIRECT,)),
                 dma, dma,

time: 23 us -> 23.7 us (1.030)
  Pallas kernels: 22.2 us -> 22.9 us
    pallas_call x1, Pallas kernels: 22.2 us -> 22.9 us  [step(): pl.pallas_call(functools.partial(kernel, n, head ** (-0.5)), out_shape=ja...]
where the time goes in v8:
time: 23.7 us; the launch traced here: 23.6 us
  Pallas kernels  22.9 us (97%)
  local copies, waits for them, and re-layouts  0.71 us (3%)
    pallas_call x1, Pallas kernels, step(): pl.pallas_call(functools.partial(kernel, n, head ** (-0.5)), out_shape=ja...  22.9 us
    unnamed x1, local copies, waits for them, and re-layouts  0.71 us

profile of v8, /device:TPU:0, one launch (start us, length us, event | category | flops | bytes accessed | tf_op | source)
XLA Modules:
  0.0 23.6 jit_solution(192105979461032659)
XLA Ops:
  0.0 22.9 %decode.1 = bf16[32,16,256]{2,1,0:T(8,128)(2,1)S(1)} custom-call(bf16[32,16,256]{2,1,0:T(8,128)(2,1)} %q_hbm.1, bf16[32,1024,256]{2,1,0:T(8,128)(2,1)} %bitcast.2, bf16[32,1024,256]{2,1,0:T(8,128)(2,1)} %bitcast.3), custom_call_target="tpu_custom_call" | custom-call | tf_op jit(solution)/shard_map/decode/pallas_call | solution.py:240
  22.9 0.7 %copy.5 = bf16[32,16,256]{2,1,0:T(8,128)(2,1)} copy(bf16[32,16,256]{2,1,0:T(8,128)(2,1)S(1)} %decode.1) | data formatting | bytes 524288

commit v9 on v7

--- a/solution.py
+++ b/solution.py
@@ -13,13 +13,13 @@
 BLOCK = 2
 PIECES = 2
 AHEAD = 5
-DIRECT = 1
+DIRECT = 3
 CUTS = (0, 6, 10)
 LANES = 128
 
 
-def kernel(n, scale, q_hbm, k_hbm, v_hbm, o_ref, q_buf, k_buf, v_buf, raw0, raw1, part, other, mine, mine_stat, theirs,
-           theirs_stat, out, q_sem, k_sem, v_sem, pair_send, pair_recv, acc_send, stat_send, acc_recv, stat_recv,
+def kernel(n, scale, q_hbm, k_hbm, v_hbm, out, q_buf, k_buf, v_buf, raw0, raw1, part, other, mine, mine_stat, theirs,
+           theirs_stat, q_sem, k_sem, v_sem, pair_send, pair_recv, acc_send, stat_send, acc_recv, stat_recv,
            direct_acc_recv, direct_stat_recv, direct_acc_recv2, direct_stat_recv2, out_send, out_recv):
     me = lax.axis_index("sp")
     chip, core = me // 2, lax.rem(me, 2)
@@ -36,7 +36,7 @@
 
     class Run:
         def __init__(self, hbm, buf, sem, b):
-            self.hbm, self.buf, self.first, self.sem = hbm, buf, b * BLOCK, sem.at[lax.rem(b, 2 * AHEAD)]
+            self.hbm, self.buf, self.first, self.sem = hbm, buf, b * BLOCK, sem.at[lax.rem(b, AHEAD)]
 
         def start(self):
             rows = tokens // PIECES
@@ -98,7 +98,10 @@
             run = slice(at, at + LANES)
             mine[t, chip, :, run] = (scale_a * a[:, run] + scale_b * b[:, run]).astype(BF16)
         both = jnp.where(lane == 0, high, total)
-        mine_stat[t, chip, :, :chips * heads] = jnp.transpose(jnp.concatenate([both] * chips, 0))[:2]
+        return jnp.transpose(jnp.concatenate([both] * chips, 0))[:2]
+
+    def keep_stat(t, rows):
+        mine_stat[t, chip, :, :chips * heads] = rows
 
     def group_of(t):
         return sum((t >= cut).astype(jnp.int32) if not isinstance(t, int) else int(t >= cut) for cut in CUTS[1:])
@@ -109,14 +112,19 @@
             remote(mine.at[t, chip], mine.at[t, chip], acc_send, acc_recv.at[group], device(r, True))
             remote(mine_stat.at[t, chip], mine_stat.at[t, chip], stat_send, stat_recv.at[group], device(r, True))
 
-    def to_all(t):
+    def acc_to_all(t):
         d = t - staged
-        for r in range(chips):
+        for r in reversed(range(chips)):
+            remote(mine.at[t, chip], theirs.at[d, chip], acc_send, direct_acc_recv2.at[d], device(r, False))
             if r > 0:
                 remote(mine.at[t, chip], mine.at[t, chip], acc_send, direct_acc_recv.at[d], device(r, True))
+
+    def stat_to_all(t):
+        d = t - staged
+        for r in reversed(range(chips)):
+            remote(mine_stat.at[t, chip], theirs_stat.at[d, chip], stat_send, direct_stat_recv2.at[d], device(r, False))
+            if r > 0:
                 remote(mine_stat.at[t, chip], mine_stat.at[t, chip], stat_send, direct_stat_recv.at[d], device(r, True))
-            remote(mine.at[t, chip], theirs.at[d, chip], acc_send, direct_acc_recv2.at[d], device(r, False))
-            remote(mine_stat.at[t, chip], theirs_stat.at[d, chip], stat_send, direct_stat_recv2.at[d], device(r, False))
 
     wide = chips * heads
     owner = lax.broadcasted_iota(jnp.int32, (1, wide), 1) // heads
@@ -141,14 +149,16 @@
             sums = jnp.dot(jnp.concatenate(terms, 0), acc[...].reshape(wide, head), preferred_element_type=F32)
             out[t, j] = (sums[:heads] + (sums[heads:2 * heads] + sums[2 * heads:])).astype(BF16)
 
+    def wait_group(g):
+        first, last = groups[g]
+        wait(mine.at[pl.ds(0, last - first), pl.ds(0, chips - 1)], acc_recv.at[g])
+        wait(mine_stat.at[pl.ds(0, last - first), pl.ds(0, chips - 1)], stat_recv.at[g])
+
     def add_group(g):
+        add_chips([(mine.at[t], mine_stat.at[t], t, core) for t in range(*groups[g])])
+
+    def send_group(g):
         first, last = groups[g]
-        count = (last - first) * (chips - 1)
-        flat = mine.at[pl.ds(0, count // (chips - 1)), pl.ds(0, chips - 1)]
-        flat_stat = mine_stat.at[pl.ds(0, count // (chips - 1)), pl.ds(0, chips - 1)]
-        wait(flat, acc_recv.at[g])
-        wait(flat_stat, stat_recv.at[g])
-        add_chips([(mine.at[t], mine_stat.at[t], t, core) for t in range(first, last)])
         run = pl.ds(first, last - first)
         remote(out.at[run, core], out.at[run, core], out_send, out_recv, device(0, False))
 
@@ -181,7 +191,7 @@
         for j in range(BLOCK):
             finish((b - 1) * BLOCK + j, raw[1 - parity].at[j])
         if first >= 4:
-            add_pair(b - 4)
+            keep_stat(b - 4, add_pair(b - 4))
 
     q_copy.wait()
     k_copy(0).wait()
@@ -200,14 +210,26 @@
     block(blocks)
     to_pair(blocks - 1)
     to_chips(blocks - 4)
-    for t in range(blocks - 3, blocks):
-        if t == blocks - 1:
-            add_group(0)
+    for t in range(blocks - 3, blocks - 1):
         wait(other.at[0], pair_recv.at[t % 8])
-        add_pair(t)
-        (to_all if t >= staged else to_chips)(t)
+    wait_group(0)
+    for t in range(blocks - 3, blocks - 1):
+        keep_stat(t, add_pair(t))
+    add_group(0)
+    for t in range(blocks - 3, blocks - 1):
+        acc_to_all(t)
+        stat_to_all(t)
+    send_group(0)
+    t = blocks - 1
+    wait(other.at[0], pair_recv.at[t % 8])
+    rows = add_pair(t)
+    acc_to_all(t)
+    keep_stat(t, rows)
+    stat_to_all(t)
     for g in range(1, len(groups)):
+        wait_group(g)
         add_group(g)
+        send_group(g)
     for d in range(DIRECT):
         wait(mine.at[0, pl.ds(0, chips - 1)], direct_acc_recv.at[d])
         wait(mine_stat.at[0, pl.ds(0, chips - 1)], direct_stat_recv.at[d])
@@ -216,9 +238,6 @@
         t = staged + d
         add_chips([(mine.at[t], mine_stat.at[t], t, core), (theirs.at[d], theirs_stat.at[d], t, 1 - core)])
     wait(out.at[pl.ds(0, staged), 0], out_recv)
-    for t in range(blocks):
-        for j in range(BLOCK):
-            o_ref[t * BLOCK + j] = out[t, j]
     wait(out.at[pl.ds(0, staged), 0], out_send)
     wait(part.at[pl.ds(0, blocks)], pair_send)
     sends = (staged * (chips - 1) + DIRECT * (n - 1)) // chips
@@ -238,7 +257,7 @@
         dma = pltpu.SemaphoreType.DMA
         return pl.pallas_call(
             functools.partial(kernel, n, head ** -0.5),
-            out_shape=jax.ShapeDtypeStruct(q.shape, BF16),
+            out_shape=jax.ShapeDtypeStruct((blocks, BLOCK, heads, head), BF16),
             in_specs=[pl.BlockSpec(memory_space=pltpu.HBM)] * 3,
             out_specs=pl.BlockSpec(memory_space=pltpu.VMEM),
             scratch_shapes=[
@@ -253,8 +272,7 @@
                 pltpu.VMEM((blocks, chips, 2, LANES), F32),
                 pltpu.VMEM((DIRECT, chips, heads, head), BF16),
                 pltpu.VMEM((DIRECT, chips, 2, LANES), F32),
-                pltpu.VMEM((blocks, BLOCK, heads, head), BF16),
-                dma, dma((2 * AHEAD,)), dma((2 * AHEAD,)),
+                dma, dma((AHEAD,)), dma((AHEAD,)),
                 dma, dma((8,)),
                 dma, dma, dma((len(CUTS),)), dma((len(CUTS),)),
                 dma((DIRECT,)), dma((DIRECT,)), dma((DIRECT,)), dma((DIRECT,)),
@@ -263,7 +281,7 @@
             compiler_params=pltpu.CompilerParams(
                 collective_id=0, has_side_effects=True, vmem_limit_bytes=48 * 1024 * 1024),
             name="decode",
-        )(pltpu.with_memory_space_constraint(q, pltpu.HBM), k, v)
+        )(pltpu.with_memory_space_constraint(q, pltpu.HBM), k, v).reshape(q.shape)
 
     return jax.shard_map(
         step,

time: 23 us -> 23.9 us (1.039)
  Pallas kernels: 22.2 us -> 23.2 us
    pallas_call x1, Pallas kernels: 22.2 us -> 23.2 us  [step(): pl.pallas_call(functools.partial(kernel, n, head ** (-0.5)), out_shape=ja...]
where the time goes in v9:
time: 23.9 us
  Pallas kernels  23.2 us (97%)
  local copies, waits for them, and re-layouts  0.71 us (3%)
    pallas_call x1, Pallas kernels, step(): pl.pallas_call(functools.partial(kernel, n, head ** (-0.5)), out_shape=ja...  23.2 us
    unnamed x1, local copies, waits for them, and re-layouts  0.71 us

profile of v9, /device:TPU:0, one launch (start us, length us, event | category | flops | bytes accessed | tf_op | source)
XLA Modules:
  0.0 23.9 jit_solution(5079686510571102502)
XLA Ops:
  0.0 23.2 %decode.1 = bf16[16,2,16,256]{3,2,1,0:T(8,128)(2,1)S(1)} custom-call(bf16[32,16,256]{2,1,0:T(8,128)(2,1)} %q_hbm.1, bf16[32,1024,256]{2,1,0:T(8,128)(2,1)} %bitcast.4, bf16[32,1024,256]{2,1,0:T(8,128)(2,1)} %bitcast.5), custom_call_target="tpu_custom_call" | custom-call | tf_op jit(solution)/shard_map/decode/pallas_call | solution.py:258
  23.2 0.7 %copy.5 = bf16[32,16,256]{2,1,0:T(8,128)(2,1)} copy(bf16[32,16,256]{2,1,0:T(8,128)(2,1)S(1)} %bitcast.3) | data formatting | bytes 524288

commit v10 on v7

--- a/solution.py
+++ b/solution.py
@@ -11,8 +11,8 @@
 F32 = jnp.float32
 BF16 = jnp.bfloat16
 BLOCK = 2
-PIECES = 2
-AHEAD = 5
+PIECES = 1
+AHEAD = 6
 DIRECT = 1
 CUTS = (0, 6, 10)
 LANES = 128

time: 23 us -> 23.1 us (level)
  no operation moved by 1% of the time
where the time goes in v10:
time: 23.1 us; the launch traced here: 23 us
  Pallas kernels  22.3 us (97%)
  local copies, waits for them, and re-layouts  0.71 us (3%)
    pallas_call x1, Pallas kernels, step(): pl.pallas_call(functools.partial(kernel, n, head ** (-0.5)), out_shape=ja...  22.3 us
    unnamed x1, local copies, waits for them, and re-layouts  0.71 us

profile of v10, /device:TPU:0, one launch (start us, length us, event | category | flops | bytes accessed | tf_op | source)
XLA Modules:
  0.0 23.0 jit_solution(15711374347015109557)
XLA Ops:
  0.0 22.3 %decode.1 = bf16[32,16,256]{2,1,0:T(8,128)(2,1)S(1)} custom-call(bf16[32,16,256]{2,1,0:T(8,128)(2,1)} %q_hbm.1, bf16[32,1024,256]{2,1,0:T(8,128)(2,1)} %bitcast.2, bf16[32,1024,256]{2,1,0:T(8,128)(2,1)} %bitcast.3), custom_call_target="tpu_custom_call" | custom-call | tf_op jit(solution)/shard_map/decode/pallas_call | solution.py:239
  22.3 0.7 %copy.5 = bf16[32,16,256]{2,1,0:T(8,128)(2,1)} copy(bf16[32,16,256]{2,1,0:T(8,128)(2,1)S(1)} %decode.1) | data formatting | bytes 524288

commit v11 on v9

--- a/solution.py
+++ b/solution.py
@@ -13,7 +13,7 @@
 BLOCK = 2
 PIECES = 2
 AHEAD = 5
-DIRECT = 3
+DIRECT = 1
 CUTS = (0, 6, 10)
 LANES = 128
 
@@ -217,8 +217,7 @@
         keep_stat(t, add_pair(t))
     add_group(0)
     for t in range(blocks - 3, blocks - 1):
-        acc_to_all(t)
-        stat_to_all(t)
+        to_chips(t)
     send_group(0)
     t = blocks - 1
     wait(other.at[0], pair_recv.at[t % 8])

time: 23.9 us -> 23.3 us (0.975)
  Pallas kernels: 23.2 us -> 22.5 us
    pallas_call x1, Pallas kernels: 23.2 us -> 22.5 us  [step(): pl.pallas_call(functools.partial(kernel, n, head ** (-0.5)), out_shape=ja...]
where the time goes in v11:
time: 23.3 us; the launch traced here: 23.2 us
  Pallas kernels  22.5 us (97%)
  local copies, waits for them, and re-layouts  0.71 us (3%)
    pallas_call x1, Pallas kernels, step(): pl.pallas_call(functools.partial(kernel, n, head ** (-0.5)), out_shape=ja...  22.5 us
    unnamed x1, local copies, waits for them, and re-layouts  0.71 us

profile of v11, /device:TPU:0, one launch (start us, length us, event | category | flops | bytes accessed | tf_op | source)
XLA Modules:
  0.0 23.2 jit_solution(15384779492339306733)
XLA Ops:
  0.0 22.5 %decode.1 = bf16[16,2,16,256]{3,2,1,0:T(8,128)(2,1)S(1)} custom-call(bf16[32,16,256]{2,1,0:T(8,128)(2,1)} %q_hbm.1, bf16[32,1024,256]{2,1,0:T(8,128)(2,1)} %bitcast.4, bf16[32,1024,256]{2,1,0:T(8,128)(2,1)} %bitcast.5), custom_call_target="tpu_custom_call" | custom-call | tf_op jit(solution)/shard_map/decode/pallas_call | solution.py:257
  22.5 0.7 %copy.5 = bf16[32,16,256]{2,1,0:T(8,128)(2,1)} copy(bf16[32,16,256]{2,1,0:T(8,128)(2,1)S(1)} %bitcast.3) | data formatting | bytes 524288

commit v12 on v7

--- a/solution.py
+++ b/solution.py
@@ -18,8 +18,8 @@
 LANES = 128
 
 
-def kernel(n, scale, q_hbm, k_hbm, v_hbm, o_ref, q_buf, k_buf, v_buf, raw0, raw1, part, other, mine, mine_stat, theirs,
-           theirs_stat, out, q_sem, k_sem, v_sem, pair_send, pair_recv, acc_send, stat_send, acc_recv, stat_recv,
+def kernel(n, scale, q_hbm, k_hbm, v_hbm, out, q_buf, k_buf, v_buf, raw0, raw1, part, other, mine, mine_stat, theirs,
+           theirs_stat, q_sem, k_sem, v_sem, pair_send, pair_recv, acc_send, stat_send, acc_recv, stat_recv,
            direct_acc_recv, direct_stat_recv, direct_acc_recv2, direct_stat_recv2, out_send, out_recv):
     me = lax.axis_index("sp")
     chip, core = me // 2, lax.rem(me, 2)
@@ -36,7 +36,7 @@
 
     class Run:
         def __init__(self, hbm, buf, sem, b):
-            self.hbm, self.buf, self.first, self.sem = hbm, buf, b * BLOCK, sem.at[lax.rem(b, 2 * AHEAD)]
+            self.hbm, self.buf, self.first, self.sem = hbm, buf, b * BLOCK, sem.at[lax.rem(b, AHEAD)]
 
         def start(self):
             rows = tokens // PIECES
@@ -169,12 +169,8 @@
                 def _():
                     k_copy(later).start()
                     v_copy(later).start()
-        if first == 2:
+        if first == 1:
             pl.semaphore_wait(barrier, n - 1)
-        if first >= 2:
-            to_pair(b - 2)
-        if first >= 5:
-            to_chips(b - 5)
         if first < blocks:
             for j in range(BLOCK):
                 scores_of(b * BLOCK + j, raw[parity].at[j])
@@ -182,6 +178,9 @@
             finish((b - 1) * BLOCK + j, raw[1 - parity].at[j])
         if first >= 4:
             add_pair(b - 4)
+        to_pair(b - 1)
+        if first >= 4:
+            to_chips(b - 4)
 
     q_copy.wait()
     k_copy(0).wait()
@@ -198,8 +197,6 @@
     lax.fori_loop(0, (blocks - 6) // 2, two, 0)
     block(blocks - 1)
     block(blocks)
-    to_pair(blocks - 1)
-    to_chips(blocks - 4)
     for t in range(blocks - 3, blocks):
         if t == blocks - 1:
             add_group(0)
@@ -216,9 +213,6 @@
         t = staged + d
         add_chips([(mine.at[t], mine_stat.at[t], t, core), (theirs.at[d], theirs_stat.at[d], t, 1 - core)])
     wait(out.at[pl.ds(0, staged), 0], out_recv)
-    for t in range(blocks):
-        for j in range(BLOCK):
-            o_ref[t * BLOCK + j] = out[t, j]
     wait(out.at[pl.ds(0, staged), 0], out_send)
     wait(part.at[pl.ds(0, blocks)], pair_send)
     sends = (staged * (chips - 1) + DIRECT * (n - 1)) // chips
@@ -238,7 +232,7 @@
         dma = pltpu.SemaphoreType.DMA
         return pl.pallas_call(
             functools.partial(kernel, n, head ** -0.5),
-            out_shape=jax.ShapeDtypeStruct(q.shape, BF16),
+            out_shape=jax.ShapeDtypeStruct((blocks, BLOCK, heads, head), BF16),
             in_specs=[pl.BlockSpec(memory_space=pltpu.HBM)] * 3,
             out_specs=pl.BlockSpec(memory_space=pltpu.VMEM),
             scratch_shapes=[
@@ -253,8 +247,7 @@
                 pltpu.VMEM((blocks, chips, 2, LANES), F32),
                 pltpu.VMEM((DIRECT, chips, heads, head), BF16),
                 pltpu.VMEM((DIRECT, chips, 2, LANES), F32),
-                pltpu.VMEM((blocks, BLOCK, heads, head), BF16),
-                dma, dma((2 * AHEAD,)), dma((2 * AHEAD,)),
+                dma, dma((AHEAD,)), dma((AHEAD,)),
                 dma, dma((8,)),
                 dma, dma, dma((len(CUTS),)), dma((len(CUTS),)),
                 dma((DIRECT,)), dma((DIRECT,)), dma((DIRECT,)), dma((DIRECT,)),
@@ -263,7 +256,7 @@
             compiler_params=pltpu.CompilerParams(
                 collective_id=0, has_side_effects=True, vmem_limit_bytes=48 * 1024 * 1024),
             name="decode",
-        )(pltpu.with_memory_space_constraint(q, pltpu.HBM), k, v)
+        )(pltpu.with_memory_space_constraint(q, pltpu.HBM), k, v).reshape(q.shape)
 
     return jax.shard_map(
         step,

time: 23 us -> 22.7 us (0.987)
  Pallas kernels: 22.2 us -> 21.9 us
    pallas_call x1, Pallas kernels: 22.2 us -> 21.9 us  [step(): pl.pallas_call(functools.partial(kernel, n, head ** (-0.5)), out_shape=ja...]
where the time goes in v12:
time: 22.7 us; the launch traced here: 22.6 us
  Pallas kernels  21.9 us (96%)
  local copies, waits for them, and re-layouts  0.71 us (3%)
    pallas_call x1, Pallas kernels, step(): pl.pallas_call(functools.partial(kernel, n, head ** (-0.5)), out_shape=ja...  21.9 us
    unnamed x1, local copies, waits for them, and re-layouts  0.71 us

profile of v12, /device:TPU:0, one launch (start us, length us, event | category | flops | bytes accessed | tf_op | source)
XLA Modules:
  0.0 22.6 jit_solution(7161087609085066555)
XLA Ops:
  0.0 21.9 %decode.1 = bf16[16,2,16,256]{3,2,1,0:T(8,128)(2,1)S(1)} custom-call(bf16[32,16,256]{2,1,0:T(8,128)(2,1)} %q_hbm.1, bf16[32,1024,256]{2,1,0:T(8,128)(2,1)} %bitcast.4, bf16[32,1024,256]{2,1,0:T(8,128)(2,1)} %bitcast.5), custom_call_target="tpu_custom_call" | custom-call | tf_op jit(solution)/shard_map/decode/pallas_call | solution.py:233
  21.9 0.7 %copy.5 = bf16[32,16,256]{2,1,0:T(8,128)(2,1)} copy(bf16[32,16,256]{2,1,0:T(8,128)(2,1)S(1)} %bitcast.3) | data formatting | bytes 524288

commit v13 on v12

--- a/solution.py
+++ b/solution.py
@@ -14,7 +14,7 @@
 PIECES = 2
 AHEAD = 5
 DIRECT = 1
-CUTS = (0, 6, 10)
+CUTS = (0, 6, 11, 13)
 LANES = 128
 
 
@@ -198,7 +198,7 @@
     block(blocks - 1)
     block(blocks)
     for t in range(blocks - 3, blocks):
-        if t == blocks - 1:
+        if t == blocks - 2:
             add_group(0)
         wait(other.at[0], pair_recv.at[t % 8])
         add_pair(t)

time: 22.7 us -> 22.7 us (level)
  no operation moved by 1% of the time
where the time goes in v13:
time: 22.7 us; the launch traced here: 22.6 us
  Pallas kernels  21.9 us (96%)
  local copies, waits for them, and re-layouts  0.71 us (3%)
    pallas_call x1, Pallas kernels, step(): pl.pallas_call(functools.partial(kernel, n, head ** (-0.5)), out_shape=ja...  21.9 us
    unnamed x1, local copies, waits for them, and re-layouts  0.71 us

profile of v13, /device:TPU:0, one launch (start us, length us, event | category | flops | bytes accessed | tf_op | source)
XLA Modules:
  0.0 22.6 jit_solution(10210369931361530968)
XLA Ops:
  0.0 21.9 %decode.1 = bf16[16,2,16,256]{3,2,1,0:T(8,128)(2,1)S(1)} custom-call(bf16[32,16,256]{2,1,0:T(8,128)(2,1)} %q_hbm.1, bf16[32,1024,256]{2,1,0:T(8,128)(2,1)} %bitcast.4, bf16[32,1024,256]{2,1,0:T(8,128)(2,1)} %bitcast.5), custom_call_target="tpu_custom_call" | custom-call | tf_op jit(solution)/shard_map/decode/pallas_call | solution.py:233
  21.9 0.7 %copy.5 = bf16[32,16,256]{2,1,0:T(8,128)(2,1)} copy(bf16[32,16,256]{2,1,0:T(8,128)(2,1)S(1)} %bitcast.3) | data formatting | bytes 524288

commit v14 on v13

--- a/solution.py
+++ b/solution.py
@@ -13,8 +13,8 @@
 BLOCK = 2
 PIECES = 2
 AHEAD = 5
-DIRECT = 1
-CUTS = (0, 6, 11, 13)
+DIRECT = 2
+CUTS = (0, 6, 10, 13)
 LANES = 128
 
 

time: 22.7 us -> 22.7 us (level)
  no operation moved by 1% of the time
where the time goes in v14:
time: 22.7 us; the launch traced here: 22.6 us
  Pallas kernels  21.9 us (96%)
  local copies, waits for them, and re-layouts  0.71 us (3%)
    pallas_call x1, Pallas kernels, step(): pl.pallas_call(functools.partial(kernel, n, head ** (-0.5)), out_shape=ja...  21.9 us
    unnamed x1, local copies, waits for them, and re-layouts  0.71 us

profile of v14, /device:TPU:0, one launch (start us, length us, event | category | flops | bytes accessed | tf_op | source)
XLA Modules:
  0.0 22.6 jit_solution(3839999543449654314)
XLA Ops:
  0.0 21.9 %decode.1 = bf16[16,2,16,256]{3,2,1,0:T(8,128)(2,1)S(1)} custom-call(bf16[32,16,256]{2,1,0:T(8,128)(2,1)} %q_hbm.1, bf16[32,1024,256]{2,1,0:T(8,128)(2,1)} %bitcast.4, bf16[32,1024,256]{2,1,0:T(8,128)(2,1)} %bitcast.5), custom_call_target="tpu_custom_call" | custom-call | tf_op jit(solution)/shard_map/decode/pallas_call | solution.py:233
  21.9 0.7 %copy.5 = bf16[32,16,256]{2,1,0:T(8,128)(2,1)} copy(bf16[32,16,256]{2,1,0:T(8,128)(2,1)S(1)} %bitcast.3) | data formatting | bytes 524288

commit v15 on v13

--- a/solution.py
+++ b/solution.py
@@ -189,12 +189,8 @@
     for b in range(1, 5):
         block(b)
 
-    def two(i, _):
-        block((2 * i + 5, 1, 5, blocks - 2))
-        block((2 * i + 6, 0, 5, blocks - 2))
-        return 0
-
-    lax.fori_loop(0, (blocks - 6) // 2, two, 0)
+    for b in range(5, blocks - 1):
+        block(b)
     block(blocks - 1)
     block(blocks)
     for t in range(blocks - 3, blocks):

time: 22.7 us -> 21.8 us (0.960)
  Pallas kernels: 21.9 us -> 21 us
    pallas_call x1, Pallas kernels: 21.9 us -> 21 us  [step(): pl.pallas_call(functools.partial(kernel, n, head ** (-0.5)), out_shape=ja...]
where the time goes in v15:
time: 21.8 us; the launch traced here: 21.7 us
  Pallas kernels  21 us (96%)
  local copies, waits for them, and re-layouts  0.71 us (3%)
    pallas_call x1, Pallas kernels, step(): pl.pallas_call(functools.partial(kernel, n, head ** (-0.5)), out_shape=ja...  21 us
    unnamed x1, local copies, waits for them, and re-layouts  0.71 us

profile of v15, /device:TPU:0, one launch (start us, length us, event | category | flops | bytes accessed | tf_op | source)
XLA Modules:
  0.0 21.7 jit_solution(12383155704319256405)
XLA Ops:
  0.0 21.0 %decode.1 = bf16[16,2,16,256]{3,2,1,0:T(8,128)(2,1)S(1)} custom-call(bf16[32,16,256]{2,1,0:T(8,128)(2,1)} %q_hbm.1, bf16[32,1024,256]{2,1,0:T(8,128)(2,1)} %bitcast.4, bf16[32,1024,256]{2,1,0:T(8,128)(2,1)} %bitcast.5), custom_call_target="tpu_custom_call" | custom-call | tf_op jit(solution)/shard_map/decode/pallas_call | solution.py:229
  21.0 0.7 %copy.5 = bf16[32,16,256]{2,1,0:T(8,128)(2,1)} copy(bf16[32,16,256]{2,1,0:T(8,128)(2,1)S(1)} %bitcast.3) | data formatting | bytes 524288

commit v16 on v15

--- a/solution.py
+++ b/solution.py
@@ -12,7 +12,7 @@
 BF16 = jnp.bfloat16
 BLOCK = 2
 PIECES = 2
-AHEAD = 5
+AHEAD = 8
 DIRECT = 1
 CUTS = (0, 6, 11, 13)
 LANES = 128

time: 21.8 us -> 23.4 us (1.073)
  Pallas kernels: 21 us -> 22.6 us
    pallas_call x1, Pallas kernels: 21 us -> 22.6 us  [step(): pl.pallas_call(functools.partial(kernel, n, head ** (-0.5)), out_shape=ja...]
where the time goes in v16:
time: 23.4 us; the launch traced here: 23.3 us
  Pallas kernels  22.6 us (97%)
  local copies, waits for them, and re-layouts  0.71 us (3%)
    pallas_call x1, Pallas kernels, step(): pl.pallas_call(functools.partial(kernel, n, head ** (-0.5)), out_shape=ja...  22.6 us
    unnamed x1, local copies, waits for them, and re-layouts  0.71 us

profile of v16, /device:TPU:0, one launch (start us, length us, event | category | flops | bytes accessed | tf_op | source)
XLA Modules:
  0.0 23.3 jit_solution(12104689310915985911)
XLA Ops:
  0.0 22.6 %decode.1 = bf16[16,2,16,256]{3,2,1,0:T(8,128)(2,1)S(1)} custom-call(bf16[32,16,256]{2,1,0:T(8,128)(2,1)} %q_hbm.1, bf16[32,1024,256]{2,1,0:T(8,128)(2,1)} %bitcast.4, bf16[32,1024,256]{2,1,0:T(8,128)(2,1)} %bitcast.5), custom_call_target="tpu_custom_call" | custom-call | tf_op jit(solution)/shard_map/decode/pallas_call | solution.py:229
  22.6 0.7 %copy.5 = bf16[32,16,256]{2,1,0:T(8,128)(2,1)} copy(bf16[32,16,256]{2,1,0:T(8,128)(2,1)S(1)} %bitcast.3) | data formatting | bytes 524288

commit v17 on v16

--- a/solution.py
+++ b/solution.py
@@ -12,7 +12,7 @@
 BF16 = jnp.bfloat16
 BLOCK = 2
 PIECES = 2
-AHEAD = 8
+AHEAD = 4
 DIRECT = 1
 CUTS = (0, 6, 11, 13)
 LANES = 128

time: 23.4 us -> 21.5 us (0.919)
  Pallas kernels: 22.6 us -> 20.7 us
    pallas_call x1, Pallas kernels: 22.6 us -> 20.7 us  [step(): pl.pallas_call(functools.partial(kernel, n, head ** (-0.5)), out_shape=ja...]
where the time goes in v17:
time: 21.5 us; the launch traced here: 21.4 us
  Pallas kernels  20.7 us (96%)
  local copies, waits for them, and re-layouts  0.71 us (3%)
    pallas_call x1, Pallas kernels, step(): pl.pallas_call(functools.partial(kernel, n, head ** (-0.5)), out_shape=ja...  20.7 us
    unnamed x1, local copies, waits for them, and re-layouts  0.71 us

profile of v17, /device:TPU:0, one launch (start us, length us, event | category | flops | bytes accessed | tf_op | source)
XLA Modules:
  0.0 21.4 jit_solution(7770395699625731047)
XLA Ops:
  0.0 20.7 %decode.1 = bf16[16,2,16,256]{3,2,1,0:T(8,128)(2,1)S(1)} custom-call(bf16[32,16,256]{2,1,0:T(8,128)(2,1)} %q_hbm.1, bf16[32,1024,256]{2,1,0:T(8,128)(2,1)} %bitcast.4, bf16[32,1024,256]{2,1,0:T(8,128)(2,1)} %bitcast.5), custom_call_target="tpu_custom_call" | custom-call | tf_op jit(solution)/shard_map/decode/pallas_call | solution.py:229
  20.7 0.7 %copy.5 = bf16[32,16,256]{2,1,0:T(8,128)(2,1)} copy(bf16[32,16,256]{2,1,0:T(8,128)(2,1)S(1)} %bitcast.3) | data formatting | bytes 524288

commit v18 on v17

--- a/solution.py
+++ b/solution.py
@@ -12,7 +12,7 @@
 BF16 = jnp.bfloat16
 BLOCK = 2
 PIECES = 2
-AHEAD = 4
+AHEAD = 3
 DIRECT = 1
 CUTS = (0, 6, 11, 13)
 LANES = 128

time: 21.5 us -> 22.5 us (1.047)
  Pallas kernels: 20.7 us -> 21.6 us
    pallas_call x1, Pallas kernels: 20.7 us -> 21.6 us  [step(): pl.pallas_call(functools.partial(kernel, n, head ** (-0.5)), out_shape=ja...]
where the time goes in v18:
time: 22.5 us; the launch traced here: 22.3 us
  Pallas kernels  21.6 us (96%)
  local copies, waits for them, and re-layouts  0.71 us (3%)
    pallas_call x1, Pallas kernels, step(): pl.pallas_call(functools.partial(kernel, n, head ** (-0.5)), out_shape=ja...  21.6 us
    unnamed x1, local copies, waits for them, and re-layouts  0.71 us

profile of v18, /device:TPU:0, one launch (start us, length us, event | category | flops | bytes accessed | tf_op | source)
XLA Modules:
  0.0 22.3 jit_solution(5003061455577738422)
XLA Ops:
  0.0 21.6 %decode.1 = bf16[16,2,16,256]{3,2,1,0:T(8,128)(2,1)S(1)} custom-call(bf16[32,16,256]{2,1,0:T(8,128)(2,1)} %q_hbm.1, bf16[32,1024,256]{2,1,0:T(8,128)(2,1)} %bitcast.4, bf16[32,1024,256]{2,1,0:T(8,128)(2,1)} %bitcast.5), custom_call_target="tpu_custom_call" | custom-call | tf_op jit(solution)/shard_map/decode/pallas_call | solution.py:229
  21.6 0.7 %copy.5 = bf16[32,16,256]{2,1,0:T(8,128)(2,1)} copy(bf16[32,16,256]{2,1,0:T(8,128)(2,1)S(1)} %bitcast.3) | data formatting | bytes 524288

commit v19 on v17

--- a/solution.py
+++ b/solution.py
@@ -12,6 +12,7 @@
 BF16 = jnp.bfloat16
 BLOCK = 2
 PIECES = 2
+FIRST = 2
 AHEAD = 4
 DIRECT = 1
 CUTS = (0, 6, 11, 13)
@@ -62,7 +63,7 @@
     q_copy = pltpu.make_async_copy(q_hbm, q_buf, q_sem)
     k_copy(0).start()
     q_copy.start()
-    for b in range(AHEAD):
+    for b in range(FIRST):
         if b > 0:
             k_copy(b).start()
         v_copy(b).start()
@@ -159,6 +160,9 @@
         v_copy(b - 1).wait()
         if first >= 4:
             wait(other.at[0], pair_recv.at[lax.rem(b - 4, 8)])
+        if b == 1:
+            k_copy(AHEAD - 1).start()
+            v_copy(AHEAD - 1).start()
         if first < blocks:
             later = b + AHEAD - 1
             if last + AHEAD - 1 < blocks:
@@ -184,6 +188,9 @@
 
     q_copy.wait()
     k_copy(0).wait()
+    for b in range(FIRST, AHEAD - 1):
+        k_copy(b).start()
+        v_copy(b).start()
     for j in range(BLOCK):
         scores_of(j, raw[0].at[j])
     for b in range(1, 5):

time: 21.5 us -> 21.1 us (0.981)
  Pallas kernels: 20.7 us -> 20.3 us
    pallas_call x1, Pallas kernels: 20.7 us -> 20.3 us  [step(): pl.pallas_call(functools.partial(kernel, n, head ** (-0.5)), out_shape=ja...]
where the time goes in v19:
time: 21.1 us; the launch traced here: 21 us
  Pallas kernels  20.3 us (96%)
  local copies, waits for them, and re-layouts  0.71 us (3%)
    pallas_call x1, Pallas kernels, step(): pl.pallas_call(functools.partial(kernel, n, head ** (-0.5)), out_shape=ja...  20.3 us
    unnamed x1, local copies, waits for them, and re-layouts  0.71 us

profile of v19, /device:TPU:0, one launch (start us, length us, event | category | flops | bytes accessed | tf_op | source)
XLA Modules:
  0.0 21.0 jit_solution(7382956632697102479)
XLA Ops:
  0.0 20.3 %decode.1 = bf16[16,2,16,256]{3,2,1,0:T(8,128)(2,1)S(1)} custom-call(bf16[32,16,256]{2,1,0:T(8,128)(2,1)} %q_hbm.1, bf16[32,1024,256]{2,1,0:T(8,128)(2,1)} %bitcast.4, bf16[32,1024,256]{2,1,0:T(8,128)(2,1)} %bitcast.5), custom_call_target="tpu_custom_call" | custom-call | tf_op jit(solution)/shard_map/decode/pallas_call | solution.py:236
  20.3 0.7 %copy.5 = bf16[32,16,256]{2,1,0:T(8,128)(2,1)} copy(bf16[32,16,256]{2,1,0:T(8,128)(2,1)S(1)} %bitcast.3) | data formatting | bytes 524288
